TPU v7x, 128 devices: a whole 4x4x4 slice. The times are simulated.
128 devices in a mesh: dp: 32 (over x, y, core), vocab: 4 (over z).
Axes of the slice: x: 4, y: 4, z: 4, core: 2. Of those that a mesh axis runs over, the one named last changes fastest.
Arguments:
- hidden_current: bfloat16 [1024, 4096], P(('dp', 'vocab'))
- hidden_proximal: bfloat16 [1024, 4096], P(('dp', 'vocab'))
- head_current: bfloat16 [4096, 128256], P(None, ('dp', 'vocab'))
- head_proximal: bfloat16 [4096, 128256], P(None, ('dp', 'vocab'))
- targets: int32 [1024], P(('dp', 'vocab')), may hold values from 0 to 128255
- loss_mask: int32 [1024], P(('dp', 'vocab')), may hold values from 0 to 1, as said below
- lengths: int32 [128], P(('dp', 'vocab')), may hold values from 1 to 8
- behavior_logprob: float32 [1024], P(('dp', 'vocab')), may hold values from -14 to -10
- advantages: float32 [1024], P(('dp', 'vocab')), may hold values from -6 to 6
Outputs:
- token_loss: float32 [1024], P(('dp', 'vocab'))
- current_logprob: float32 [1024], P(('dp', 'vocab'))
- stats: float32 [3], replicated
Inputs may be any that keep to these rules, and one draw needn't show every extreme that they name: `loss_mask`: 1 at the first position of every sequence's window.
All inputs are finite; a program needn't handle non-finite values.
Results may differ from a plain program's by a relative error of at most 0.0003.
Values may be sent and summed in bfloat16 or wider, within the bound.
No kernel may reach another device: no remote copies, remote signals or barrier semaphores. Data moves between devices by JAX's collectives and lax.ppermute only.
A program may use at most 128 MiB of HBM per device.

v0:
```python
import jax
import jax.numpy as jnp
from jax import lax
from jax.sharding import Mesh
from jax.sharding import PartitionSpec as P

POSITIONS = 8
DP_VOCAB = ("dp_0", "dp_1", "dp_2", "vocab")
CLIP_EPS = 0.2
WEIGHT_CAP = 5.0


def joined_along(blocks, dim):
    lengths = list(blocks.shape[1:])
    lengths[dim] *= blocks.shape[0]
    return jnp.moveaxis(blocks, 0, dim).reshape(lengths)


def gather_in_order(x, axes, turns):
    blocks = x
    for k in turns:
        blocks = lax.all_gather(blocks, axes[k])
    done = turns[::-1]
    back = [done.index(k) for k in range(len(axes))]
    blocks = blocks.transpose(*back, *range(len(axes), blocks.ndim))
    return blocks.reshape(-1, *x.shape)


def gather_axes(x, axes, turns, dim):
    return joined_along(gather_in_order(x, axes, turns), dim)


def rows_first(arrays, axis, dims):
    turned = [jnp.moveaxis(a, dim, 0) for a, dim in zip(arrays, dims)]
    widths = [t[0].size for t in turned]
    both = jnp.concatenate([t.reshape(-1, w) for t, w in zip(turned, widths)], axis=1)
    result = lax.all_gather(both, axis, axis=0, tiled=True)
    blocks = jnp.split(result, [sum(widths[:k]) for k in range(1, len(widths))], axis=1)
    return tuple(
        (
            jnp.moveaxis(b.reshape(-1, *t.shape[1:]), 0, dim)
            for b, t, dim in zip(blocks, turned, dims)
        )
    )


def all_in_one(x, axis):
    leaves = jax.tree.leaves(x)
    turns = sorted(range(len(leaves)), key=lambda k: -leaves[k].size)
    width = (1, *leaves[turns[0]].shape)[-1]
    lines = [
        jnp.pad(leaves[k].reshape(-1), (0, -leaves[k].size % width)).reshape(-1, width)
        for k in turns
    ]
    both, at, found = (lax.all_gather(jnp.concatenate(lines), axis), 0, {})
    for k, line in zip(turns, lines):
        piece = both[:, at : at + len(line)].reshape(len(both), -1)
        found[k] = piece[:, : leaves[k].size].reshape(-1, *leaves[k].shape)
        at += len(line)
    numbers = iter(range(len(leaves)))
    return jax.tree.map(lambda _: found[next(numbers)], x)


def combined_by_axis(x, axes, combine):
    for axis in axes:
        pieces = all_in_one(x, axis)
        x = jax.tree.map(lambda part: part[0], pieces)
        for k in range(1, lax.axis_size(axis)):
            x = combine(x, jax.tree.map(lambda part: part[k], pieces))
    return x


def column_stats(logits, wanted, first_col, with_entropy):
    peak = jnp.max(logits, axis=1)
    weights = jnp.exp(logits - peak[:, None])
    total = jnp.sum(weights, axis=1)
    columns = first_col + lax.broadcasted_iota(jnp.int32, logits.shape, 1)
    picked = jnp.sum(jnp.where(columns == wanted[:, None], logits, jnp.float32(0.0)), axis=1)
    if with_entropy:
        moment = jnp.sum(weights * logits, axis=1)
        return [peak, total, moment, picked]
    return [peak, total, picked]


def token_terms(logp_current, logp_proximal, entropy, advantages, behavior, live):
    ratio = jnp.exp(logp_current - logp_proximal)
    clipped = jnp.clip(ratio, 1.0 - CLIP_EPS, 1.0 + CLIP_EPS)
    surrogate = jnp.maximum(-advantages * ratio, -advantages * clipped)
    weight = jnp.minimum(jnp.exp(logp_proximal - behavior), WEIGHT_CAP)
    return (surrogate * weight * live, weight * live, entropy * live)


def merge_rows(first, second):
    peak_c = jnp.maximum(first[0], second[0])
    fa_c = jnp.exp(first[0] - peak_c)
    fb_c = jnp.exp(second[0] - peak_c)
    peak_p = jnp.maximum(first[4], second[4])
    fa_p = jnp.exp(first[4] - peak_p)
    fb_p = jnp.exp(second[4] - peak_p)
    return (
        peak_c,
        first[1] * fa_c + second[1] * fb_c,
        first[2] * fa_c + second[2] * fb_c,
        first[3] + second[3],
        peak_p,
        first[5] * fa_p + second[5] * fb_p,
        first[6] + second[6],
    )


def local(
    hidden_current,
    hidden_proximal,
    head_current,
    head_proximal,
    targets,
    loss_mask,
    lengths,
    behavior_logprob,
    advantages,
):
    tok_dev = targets.shape[0]
    first_col = lax.axis_index(DP_VOCAB) * head_current.shape[1]
    row_start = lax.axis_index(DP_VOCAB) * tok_dev
    all_targets = gather_axes(targets, DP_VOCAB, (0, 1, 3, 2), 0)
    place = lax.broadcasted_iota(jnp.int32, (lengths.shape[0], POSITIONS), 1)
    live = ((place < lengths[:, None]).reshape(-1) & (loss_mask == 1)).astype(jnp.float32)
    spread_adv, spread_behav, spread_live = rows_first(
        (advantages, behavior_logprob, live), DP_VOCAB, (0, 0, 0)
    )
    stacked = jnp.stack([hidden_current, hidden_proximal])
    pieces = lax.all_gather(stacked, DP_VOCAB, axis=1, tiled=True)
    logits = jnp.dot(pieces[0], head_current, preferred_element_type=jnp.float32)
    proximal_logits = jnp.dot(pieces[1], head_proximal, preferred_element_type=jnp.float32)
    stats = jnp.concatenate(
        [
            jnp.stack(column_stats(logits, all_targets, first_col, True)),
            jnp.stack(column_stats(proximal_logits, all_targets, first_col, False)),
        ],
        axis=0,
    )
    peak_c, total_c, moment_c, picked_c, peak_p, total_p, picked_p = combined_by_axis(
        (stats[0], stats[1], stats[2], stats[3], stats[4], stats[5], stats[6]), DP_VOCAB, merge_rows
    )
    lse_c = peak_c + jnp.log(total_c)
    logp_c = picked_c - lse_c
    entropy = lse_c - moment_c / total_c
    logp_p = picked_p - (peak_p + jnp.log(total_p))

    def mine(values):
        return lax.dynamic_slice_in_dim(values, row_start, tok_dev)

    loss_all, weight_all, ent_all = token_terms(
        logp_c, logp_p, entropy, spread_adv, spread_behav, spread_live
    )
    loss_sum = jnp.sum(loss_all)
    weight_sum = jnp.sum(weight_all)
    ent_sum = jnp.sum(ent_all)
    count = jnp.sum(spread_live)
    token_loss = mine(loss_all)
    summary = jnp.stack([loss_sum / count, weight_sum / count, ent_sum / count])
    return (token_loss, mine(logp_c), summary)


def solution(mesh):
    torus = Mesh(
        mesh.devices.reshape(4, 4, 2, mesh.shape["vocab"]), ("dp_0", "dp_1", "dp_2", "vocab")
    )
    return jax.shard_map(
        local,
        mesh=torus,
        in_specs=(
            P(DP_VOCAB, None),
            P(DP_VOCAB, None),
            P(None, DP_VOCAB),
            P(None, DP_VOCAB),
            P(DP_VOCAB),
            P(DP_VOCAB),
            P(DP_VOCAB),
            P(DP_VOCAB),
            P(DP_VOCAB),
        ),
        out_specs=(P(DP_VOCAB), P(DP_VOCAB), P()),
        check_vma=False,
    )
```

profile of v0, /device:TPU:0, one launch (start us, length us, event | category | flops | bytes accessed | tf_op | source)
XLA Modules:
  0.0 191.8 jit_solution(17642314294990038285)
XLA Ops:
  7.2 1.5 pad_maximum_fusion
  8.8 1.2 dynamic-slice
  10.7 0.9 dynamic-update-slice
  11.5 9.0 %all-reduce = s32[32]{0:T(128)S(1)} all-reduce(s32[32]{0:T(128)S(1)} %dynamic-update-slice), channel_id=2, replica_groups=mesh['dp_0'=4,'dp_1'=4,'dp_2'=2,'vocab'=4] {'dp_0'}, use_global_device_ids=true, to_apply=%add | all-reduce | flops 32 | bytes 256
  20.6 11.3 %all-gather.9 = s32[4,4,8]{2,1,0:T(4,128)S(1)} all-gather(s32[1,4,8]{2,1,0:T(4,128)S(1)} %reshape.1551), channel_id=3, replica_groups=mesh['dp_0'=4,'dp_1'=4,'dp_2'=2,'vocab'=4] {'dp_1'}, dimensions={0}, use_global_device_ids=true | all-gather | bytes 640 | tf_op jit(solution)/shard_map/all_gather | solution.py:22
  31.9 13.1 %all-gather.2 = s32[16,4,8]{2,1,0:T(4,128)S(1)} all-gather(s32[4,4,8]{2,1,0:T(4,128)S(1)} %all-gather.9), channel_id=4, replica_groups=mesh['dp_0'=4,'dp_1'=4,'dp_2'=2,'vocab'=4] {'vocab'}, dimensions={0}, use_global_device_ids=true | all-gather | bytes 2560 | tf_op jit(solution)/shard_map/all_gather | solution.py:22
  45.0 1.8 all-gather.3
  47.7 0.7 fusion.95
  48.3 0.7 maximum_bitcast_fusion
  49.0 61.3 %all-gather.8 = f32[128,8,3]{1,2,0:T(4,128)S(1)} all-gather(f32[1,8,3]{1,2,0:T(4,128)S(1)} %maximum_bitcast_fusion), channel_id=1, replica_groups=mesh['dp_0'=4,'dp_1'=4,'dp_2'=2,'vocab'=4] {'dp_0','dp_1','dp_2','vocab'}, dimensions={0}, use_global_device_ids=true | all-gather | bytes 12384 | tf_op jit(solution)/shard_map/all_gather | solution.py:37
  110.3 0.1 reshape.1550
  110.5 0.6 slice_reduce_fusion
  111.1 12.8 %fusion.106 = (f32[1024]{0:T(1024)S(1)}, f32[1024,1002]{0,1:T(8,128)S(1)}) fusion(bf16[4096,1002]{0,1:T(8,128)(2,1)} %param.11, bf16[2,1024,4096]{2,1,0:T(8,128)(2,1)} %all-gather.16.cloned.1.call-done), kind=kOutput, calls=%fused_computation.216 | convolution fusion | flops 8406410240 | bytes 20754432 | tf_op jit(solution)/shard_map/dot_general | solution.py:133
  123.9 12.8 %fusion.107 = (f32[1024]{0:T(1024)S(1)}, f32[1024,1002]{0,1:T(8,128)S(1)}) fusion(bf16[4096,1002]{0,1:T(8,128)(2,1)} %param.12, bf16[2,1024,4096]{2,1,0:T(8,128)(2,1)} %all-gather.16.cloned.1.call-done), kind=kOutput, calls=%fused_computation.217 | convolution fusion | flops 8406410240 | bytes 20754432 | tf_op jit(solution)/shard_map/dot_general | solution.py:134
  136.7 2.5 %fusion.3 = (f32[1024]{0:T(1024)S(1)}, f32[1024]{0:T(1024)S(1)}, f32[1024]{0:T(1024)S(1)}, f32[1024]{0:T(1024)S(1)}, f32[1024]{0:T(1024)S(1)}) fusion(f32[1024,1002]{0,1:T(8,128)S(1)} %get-tuple-element.69, s32[1024]{0:T(1024)S(1)} %eq.18, s32[1002]{0:T(1024)S(1)} %iota_add_fusion, f32[1024]{0:T(1024)S(1)} %get-tuple-element.68, ...), kind=kLoop, calls=%fused_computation.7 | loop fusion | flops 11281408 | bytes 8245160 | tf_op jit(solution)/shard_map/reduce_sum | solution.py:78
  139.3 12.0 %all-gather.10 = f32[4,7,1024]{2,1,0:T(8,128)S(1)} all-gather(f32[1,7,1024]{2,1,0:T(8,128)S(1)} %bitcast.552), channel_id=6, replica_groups=mesh['dp_0'=4,'dp_1'=4,'dp_2'=2,'vocab'=4] {'dp_0'}, dimensions={0}, use_global_device_ids=true | all-gather | bytes 143360 | tf_op jit(solution)/shard_map/all_gather | solution.py:55
  151.5 12.0 %all-gather.11 = f32[4,7,1024]{2,1,0:T(8,128)S(1)} all-gather(f32[1,7,1024]{2,1,0:T(8,128)S(1)} %bitcast.553), channel_id=7, replica_groups=mesh['dp_0'=4,'dp_1'=4,'dp_2'=2,'vocab'=4] {'dp_1'}, dimensions={0}, use_global_device_ids=true | all-gather | bytes 143360 | tf_op jit(solution)/shard_map/all_gather | solution.py:55
  163.8 1.9 all-gather.12
  165.8 12.0 %all-gather.13 = f32[4,7,1024]{2,1,0:T(8,128)S(1)} all-gather(f32[1,7,1024]{2,1,0:T(8,128)S(1)} %bitcast.555), channel_id=9, replica_groups=mesh['dp_0'=4,'dp_1'=4,'dp_2'=2,'vocab'=4] {'vocab'}, dimensions={0}, use_global_device_ids=true | all-gather | bytes 143360 | tf_op jit(solution)/shard_map/all_gather | solution.py:55
  177.9 0.6 fusion.96
  179.9 0.6 multiply_reduce_fusion.2
  183.2 0.6 dynamic_slice.7
  183.8 0.6 dynamic_slice.6
  184.4 0.6 pad_maximum_fusion.1
  (24 shorter events, 1.0 us)
Async XLA Ops:
  7.2 103.9 %all-gather.16.cloned.1.call-start = ((), (), s32[]{:S(2)}) async-start(), calls=%async_computation | async-start | bytes 16908288 | tf_op jit(solution)/shard_map/all_gather | solution.py:132
Sparse Core Ops, SparseCore 0:
  11.0 83.1 all-gather.15
where the time goes:
time: 192 us
  blocking collectives  134 us (70%)
  matrix products  25.6 us (13%)
  between operations  19.5 us (10%)
  other arithmetic  8.41 us (4%)
  local copies, waits for them, and re-layouts  3.87 us (2%)
    all_gather x1, blocking collectives, rows_first(): result = lax.all_gather(both, axis, axis=0, tiled=True)  61.3 us
    all_gather x4, blocking collectives, all_in_one(): both, at, found = (lax.all_gather(jnp.concatenate(lines), axis), 0, {})  37.8 us
    all_gather x3, blocking collectives, gather_in_order(): blocks = lax.all_gather(blocks, axes[k])  26.3 us
    dot_general x1, matrix products, local(): jnp.dot(pieces[1], head_proximal, preferred_element_type=jnp.float32)  12.8 us
    dot_general x1, matrix products, local(): jnp.dot(pieces[0], head_current, preferred_element_type=jnp.float32)  12.8 us
    unnamed x1, blocking collectives  8.99 us
  transfers between devices with their start and end apart: 1, of which 0 were waited for; matrix products, arithmetic and copies ran while one was open for 2% of the time, Pallas kernels for 0%

commit v1 on v0

--- a/solution.py
+++ b/solution.py
@@ -34,7 +34,10 @@
     turned = [jnp.moveaxis(a, dim, 0) for a, dim in zip(arrays, dims)]
     widths = [t[0].size for t in turned]
     both = jnp.concatenate([t.reshape(-1, w) for t, w in zip(turned, widths)], axis=1)
-    result = lax.all_gather(both, axis, axis=0, tiled=True)
+    size = lax.axis_size(axis)
+    parts = jnp.stack([both for _ in range(size)])
+    parts = lax.all_to_all(parts, axis, split_axis=0, concat_axis=0)
+    result = jnp.concatenate(parts, axis=0)
     blocks = jnp.split(result, [sum(widths[:k]) for k in range(1, len(widths))], axis=1)
     return tuple(
         (

time: 192 us -> 176 us (0.917)
  blocking collectives: 134 us -> 72.8 us
  waiting for transfers between devices: 0.02 us -> 33.8 us
  starting transfers between devices: 0.04 us -> 11.2 us
    all_gather x1 -> x0, blocking collectives: 61.3 us -> none  [rows_first(): result = lax.all_gather(both, axis, axis=0, tiled=True)]
    all_gather x1, waiting for transfers between devices: 0.01 us -> 33.7 us  [local(): pieces = lax.all_gather(stacked, DP_VOCAB, axis=1, tiled=True)]
    all_to_all x0 -> x1, starting transfers between devices: none -> 11.2 us  [rows_first(): parts = lax.all_to_all(parts, axis, split_axis=0, concat_axis=0)]
  transfers between devices with their start and end apart: 1 -> 2, of which waited for: 0 -> 1; matrix products, arithmetic and copies ran while one was open for 2% -> 3% of each run, Pallas kernels for 0% -> 0%
where the time goes in v1:
time: 176 us
  blocking collectives  72.8 us (41%)
  waiting for transfers between devices  33.8 us (19%)
  matrix products  25.6 us (15%)
  between operations  19.5 us (11%)
  starting transfers between devices  11.2 us (6%)
  other arithmetic  8.43 us (5%)
  local copies, waits for them, and re-layouts  4.61 us (3%)
    all_gather x4, blocking collectives, all_in_one(): both, at, found = (lax.all_gather(jnp.concatenate(lines), axis), 0, {})  38.7 us
    all_gather x1, waiting for transfers between devices, local(): pieces = lax.all_gather(stacked, DP_VOCAB, axis=1, tiled=True)  33.7 us
    all_gather x3, blocking collectives, gather_in_order(): blocks = lax.all_gather(blocks, axes[k])  25.7 us
    dot_general x1, matrix products, local(): jnp.dot(pieces[1], head_proximal, preferred_element_type=jnp.float32)  12.8 us
    dot_general x1, matrix products, local(): jnp.dot(pieces[0], head_current, preferred_element_type=jnp.float32)  12.8 us
    all_to_all x1, starting transfers between devices, rows_first(): parts = lax.all_to_all(parts, axis, split_axis=0, concat_axis=0)  11.2 us
    unnamed x1, blocking collectives  8.32 us
  transfers between devices with their start and end apart: 2, of which 1 were waited for; matrix products, arithmetic and copies ran while one was open for 3% of the time, Pallas kernels for 0%

profile of v1, /device:TPU:0, one launch (start us, length us, event | category | flops | bytes accessed | tf_op | source)
XLA Modules:
  0.0 175.9 jit_solution(18194553068011569381)
XLA Ops:
  7.2 1.5 pad_maximum_fusion
  9.4 0.7 fusion.95
  10.1 0.7 pad_maximum_fusion.1
  10.8 0.7 stack.16
  11.5 11.2 %all-to-all-start = ((f32[128,8,3]{1,2,0:T(4,128)}), f32[128,8,3]{1,2,0:T(4,128)S(1)}, u32[]{:S(2)}, u32[]{:S(2)}) async-start(f32[128,8,3]{1,2,0:T(4,128)} %stack.16), calls=%async_computation | async-start | bytes 524288 | tf_op jit(solution)/shard_map/all_to_all | solution.py:39
  22.7 1.2 dynamic-slice
  24.6 0.9 dynamic-update-slice
  25.5 8.3 %all-reduce = s32[32]{0:T(128)S(1)} all-reduce(s32[32]{0:T(128)S(1)} %dynamic-update-slice), channel_id=2, replica_groups=mesh['dp_0'=4,'dp_1'=4,'dp_2'=2,'vocab'=4] {'dp_0'}, use_global_device_ids=true, to_apply=%add | all-reduce | flops 32 | bytes 256
  33.9 11.1 %all-gather.8 = s32[4,4,8]{2,1,0:T(4,128)S(1)} all-gather(s32[1,4,8]{2,1,0:T(4,128)S(1)} %reshape.1555), channel_id=3, replica_groups=mesh['dp_0'=4,'dp_1'=4,'dp_2'=2,'vocab'=4] {'dp_1'}, dimensions={0}, use_global_device_ids=true | all-gather | bytes 640 | tf_op jit(solution)/shard_map/all_gather | solution.py:22
  45.0 12.7 %all-gather.2 = s32[16,4,8]{2,1,0:T(4,128)S(1)} all-gather(s32[4,4,8]{2,1,0:T(4,128)S(1)} %all-gather.8), channel_id=4, replica_groups=mesh['dp_0'=4,'dp_1'=4,'dp_2'=2,'vocab'=4] {'vocab'}, dimensions={0}, use_global_device_ids=true | all-gather | bytes 2560 | tf_op jit(solution)/shard_map/all_gather | solution.py:22
  57.7 1.8 %all-gather.3 = s32[8,4,4,8]{3,2,1,0:T(4,128)S(1)} all-gather(s32[4,4,4,8]{3,2,1,0:T(4,128)S(1)} %bitcast.549), channel_id=5, replica_groups=mesh['dp_0'=4,'dp_1'=4,'dp_2'=2,'vocab'=4] {'dp_2'}, dimensions={0}, use_global_device_ids=true | all-gather | bytes 6144 | tf_op jit(solution)/shard_map/all_gather | solution.py:22
  59.9 0.6 slice_reduce_fusion
  60.5 33.7 %all-gather.15.cloned.1.call-done = bf16[2,1024,4096]{2,1,0:T(8,128)(2,1)} async-done(((bf16[2,8,4096]{2,1,0:T(8,128)(2,1)}), bf16[2,1024,4096]{2,1,0:T(8,128)(2,1)}) %all-gather.15.cloned.1.call-update) | async-done | bytes 16777232 | tf_op jit(solution)/shard_map/all_gather | solution.py:135
  94.3 12.8 %fusion.106 = (f32[1024]{0:T(1024)S(1)}, f32[1024,1002]{0,1:T(8,128)S(1)}) fusion(bf16[4096,1002]{0,1:T(8,128)(2,1)} %param.11, bf16[2,1024,4096]{2,1,0:T(8,128)(2,1)} %all-gather.15.cloned.1.call-done), kind=kOutput, calls=%fused_computation.216 | convolution fusion | flops 8406410240 | bytes 20754432 | tf_op jit(solution)/shard_map/dot_general | solution.py:136
  107.1 12.8 %fusion.107 = (f32[1024]{0:T(1024)S(1)}, f32[1024,1002]{0,1:T(8,128)S(1)}) fusion(bf16[4096,1002]{0,1:T(8,128)(2,1)} %param.12, bf16[2,1024,4096]{2,1,0:T(8,128)(2,1)} %all-gather.15.cloned.1.call-done), kind=kOutput, calls=%fused_computation.217 | convolution fusion | flops 8406410240 | bytes 20754432 | tf_op jit(solution)/shard_map/dot_general | solution.py:137
  119.9 2.5 %fusion.3 = (f32[1024]{0:T(1024)S(1)}, f32[1024]{0:T(1024)S(1)}, f32[1024]{0:T(1024)S(1)}, f32[1024]{0:T(1024)S(1)}, f32[1024]{0:T(1024)S(1)}) fusion(f32[1024,1002]{0,1:T(8,128)S(1)} %get-tuple-element.69, s32[1024]{0:T(1024)S(1)} %eq.18, s32[1002]{0:T(1024)S(1)} %iota_add_fusion, f32[1024]{0:T(1024)S(1)} %get-tuple-element.68, ...), kind=kLoop, calls=%fused_computation.7 | loop fusion | flops 11281408 | bytes 8245160 | tf_op jit(solution)/shard_map/reduce_sum | solution.py:81
  122.5 12.3 %all-gather.9 = f32[4,7,1024]{2,1,0:T(8,128)S(1)} all-gather(f32[1,7,1024]{2,1,0:T(8,128)S(1)} %bitcast.550), channel_id=6, replica_groups=mesh['dp_0'=4,'dp_1'=4,'dp_2'=2,'vocab'=4] {'dp_0'}, dimensions={0}, use_global_device_ids=true | all-gather | bytes 143360 | tf_op jit(solution)/shard_map/all_gather | solution.py:58
  135.0 12.5 %all-gather.10 = f32[4,7,1024]{2,1,0:T(8,128)S(1)} all-gather(f32[1,7,1024]{2,1,0:T(8,128)S(1)} %bitcast.551), channel_id=7, replica_groups=mesh['dp_0'=4,'dp_1'=4,'dp_2'=2,'vocab'=4] {'dp_1'}, dimensions={0}, use_global_device_ids=true | all-gather | bytes 143360 | tf_op jit(solution)/shard_map/all_gather | solution.py:58
  147.7 1.9 %all-gather.11 = f32[2,7,1024]{2,1,0:T(8,128)S(1)} all-gather(f32[1,7,1024]{2,1,0:T(8,128)S(1)} %bitcast.552), channel_id=8, replica_groups=mesh['dp_0'=4,'dp_1'=4,'dp_2'=2,'vocab'=4] {'dp_2'}, dimensions={0}, use_global_device_ids=true | all-gather | bytes 86016 | tf_op jit(solution)/shard_map/all_gather | solution.py:58
  149.7 12.1 %all-gather.12 = f32[4,7,1024]{2,1,0:T(8,128)S(1)} all-gather(f32[1,7,1024]{2,1,0:T(8,128)S(1)} %bitcast.553), channel_id=9, replica_groups=mesh['dp_0'=4,'dp_1'=4,'dp_2'=2,'vocab'=4] {'vocab'}, dimensions={0}, use_global_device_ids=true | all-gather | bytes 143360 | tf_op jit(solution)/shard_map/all_gather | solution.py:58
  162.0 0.6 fusion.96
  164.0 0.6 multiply_reduce_fusion.2
  167.3 0.6 dynamic_slice.7
  168.4 0.6 pad_maximum_fusion.2
  (26 shorter events, 1.8 us)
Async XLA Ops:
  7.2 87.1 %all-gather.15.cloned.1.call-start = ((), (), s32[]{:S(2)}) async-start(), calls=%async_computation.1 | async-start | bytes 16908288 | tf_op jit(solution)/shard_map/all_gather | solution.py:135
  11.5 48.2 %all-to-all-start = ((f32[128,8,3]{1,2,0:T(4,128)}), f32[128,8,3]{1,2,0:T(4,128)S(1)}, u32[]{:S(2)}, u32[]{:S(2)}) async-start(f32[128,8,3]{1,2,0:T(4,128)} %stack.16), calls=%async_computation | async-start | bytes 524288 | tf_op jit(solution)/shard_map/all_to_all | solution.py:39
Sparse Core Ops, SparseCore 0:
  11.0 83.2 all-gather.14
